TPU v7x, 32 devices: a whole 2x2x4 slice. The times are simulated.
32 devices in a mesh: col: 4 (over y, core), row: 8 (over z, x).
Axes of the slice: x: 2, y: 2, z: 4, core: 2. Of those that a mesh axis runs over, the one named last changes fastest.
Arguments:
- column_table: float32 [32768, 512], P('row', 'col'), may hold values from -3 to 3
- bag_rows: int32 [256, 32], P('row'), may hold values from 0 to 32767
Outputs:
- row_table: float32 [8, 4096, 512], P(None, ('col', 'row'))
- pooled: float32 [256, 512], P('row', 'col')
Inputs may be any that keep to these rules, and one draw needn't show every extreme that they name: `bag_rows`: row indices of the table; a few rows are named far more often than the rest.
All inputs are finite; a program needn't handle non-finite values.
Results may differ from a plain program's by a relative error of at most 0.000078.
Values sent between devices are 32-bit elements; how exact they have to be, the bound alone decides.
No kernel may reach another device: no remote copies, remote signals or barrier semaphores. Data moves between devices by JAX's collectives and lax.ppermute only.
A program may use at most 64 MiB of HBM per device.

v0:
```python
import math

import jax
import jax.numpy as jnp
from jax import lax
from jax.sharding import PartitionSpec as P


def pooling(positions, table_rows):
    row_count = table_rows.shape[0]
    bag_count = positions.shape[0]
    block_rows = math.gcd(row_count, 512)
    turns = row_count // block_rows
    running = jnp.zeros((bag_count, table_rows.shape[1]), jnp.float32)
    tile_ids = jnp.arange(block_rows, dtype=jnp.int32)

    def advance(turn, carried):
        offset = turn * block_rows
        within = positions - offset
        matches = within[:, :, None] == tile_ids[None, None, :]
        counts = jnp.sum(matches.astype(jnp.float32), axis=1)
        table_block = lax.dynamic_slice_in_dim(table_rows, offset, block_rows, 0)
        return carried + jnp.dot(
            counts, table_block, precision=lax.Precision.HIGHEST, preferred_element_type=jnp.float32
        )

    return lax.fori_loop(0, turns, advance, running)


def per_device(column_table, bag_rows):
    row_groups = lax.axis_size("row")
    col_groups = lax.axis_size("col")
    block_len, col_width = column_table.shape
    full_width = col_width * col_groups
    span = block_len // (col_groups * row_groups)
    row_index = lax.axis_index("row")
    every_bag = lax.all_gather(bag_rows, "row", axis=0, tiled=True)
    sectioned = column_table.reshape(col_groups, row_groups, span, col_width)
    moved = lax.all_to_all(
        lax.all_to_all(sectioned, "col", split_axis=0, concat_axis=3, tiled=True),
        "row",
        split_axis=1,
        concat_axis=0,
        tiled=True,
    )
    row_table = moved.reshape(row_groups, span, full_width)
    first_row = row_index * block_len
    shifted = every_bag - first_row
    inside = (shifted >= 0) & (shifted < block_len)
    positions = jnp.where(inside, shifted, -1)
    pooled = lax.psum_scatter(
        pooling(positions, column_table), "row", scatter_dimension=0, tiled=True
    )
    return (row_table, pooled)


def solution(mesh):
    return jax.shard_map(
        per_device,
        mesh=mesh,
        in_specs=(P("row", "col"), P("row", None)),
        out_specs=(P(None, ("col", "row"), None), P("row", "col")),
        check_vma=False,
    )
```

profile of v0, /device:TPU:0, one launch (start us, length us, event | category | flops | bytes accessed | tf_op | source)
XLA Modules:
  0.0 161.4 jit_solution(9347695507978795825)
XLA Ops:
  7.2 4.3 %all-to-all-start = ((f32[4,8,128,128]{3,2,1,0:T(8,128)}), f32[4,8,128,128]{3,2,1,0:T(8,128)S(1)}, u32[]{:S(2)}, u32[]{:S(2)}) async-start(f32[4,8,128,128]{3,2,1,0:T(8,128)} %bitcast.12), calls=%async_computation | async-start | bytes 4194304 | tf_op jit(solution)/shard_map/all_to_all | solution.py:40
  11.5 31.8 %all_gather.3 = s32[256,32]{1,0:T(8,128)S(1)} all-gather(s32[32,32]{1,0:T(8,128)S(1)} %copy-done.1), channel_id=1, replica_groups=mesh['col'=4,'row'=8] {'row'}, dimensions={0}, use_global_device_ids=true | all-gather | bytes 36864 | tf_op jit(solution)/shard_map/all_gather | solution.py:37
  43.3 1.8 %copy.7 = f32[4,8,128,128]{2,3,0,1:T(8,128)} copy(f32[4,8,128,128]{3,2,1,0:T(8,128)S(1)} %all-to-all-done) | data formatting | bytes 4194304 | tf_op jit(solution)/shard_map/all_to_all | solution.py:40
  45.1 2.9 %copy.8 = f32[1,8,128,512]{3,2,0,1:T(8,128)} copy(f32[1,8,128,512]{2,3,1,0:T(8,128)} %bitcast.11) | data formatting | bytes 4194304 | tf_op jit(solution)/shard_map/all_to_all | solution.py:40
  48.0 5.4 %all-to-all-start.1 = ((f32[1,8,128,512]{3,2,0,1:T(8,128)}), f32[1,8,128,512]{3,2,0,1:T(8,128)S(1)}, u32[]{:S(2)}, u32[]{:S(2)}) async-start(f32[1,8,128,512]{3,2,0,1:T(8,128)} %copy.8), calls=%async_computation.1 | async-start | bytes 4194304 | tf_op jit(solution)/shard_map/all_to_all | solution.py:39
  53.4 35.3 %while.14 = (s32[]{:T(128)}, f32[256,128]{1,0:T(8,128)S(1)}, s32[256,32]{1,0:T(8,128)S(1)}, f32[4096,128]{1,0:T(8,128)}, s32[]{:T(128)}, /*index=5*/s32[]{:T(128)}, s32[]{:T(128)}, s32[]{:T(128)}) while((s32[]{:T(128)}, f32[256,128]{1,0:T(8,128)S(1)}, s32[256,32]{1,0:T(8,128)S(1)}, f32[4096,128]{1,0:T(8,128)}, s32[]{:T(128)}, ...), condition=%wide.region_2.3_spmd.clone, body=%wide.region_0.2_spmd.clone.sunk | while | flops 213852160 | bytes 1671317 | solution.py:27
  53.5 2.8 %convert_reduce_fusion.2 = f32[256,512]{1,0:T(8,128)S(1)} fusion(s32[256,32]{1,0:T(8,128)S(1)} %broadcast_subtract_fusion.2), kind=kLoop, calls=%fused_computation.2.clone.1 | loop fusion | flops 12451840 | bytes 557056 | tf_op jit(solution)/shard_map/while/body/eval_jaxpr/reduce_sum | solution.py:21
  56.3 1.6 convolution_add_fusion.2
  57.9 2.8 %convert_reduce_fusion.2 = f32[256,512]{1,0:T(8,128)S(1)} fusion(s32[256,32]{1,0:T(8,128)S(1)} %broadcast_subtract_fusion.2), kind=kLoop, calls=%fused_computation.2.clone.1 | loop fusion | flops 12451840 | bytes 557056 | tf_op jit(solution)/shard_map/while/body/eval_jaxpr/reduce_sum | solution.py:21
  60.7 1.6 convolution_add_fusion.2
  62.3 2.8 %convert_reduce_fusion.2 = f32[256,512]{1,0:T(8,128)S(1)} fusion(s32[256,32]{1,0:T(8,128)S(1)} %broadcast_subtract_fusion.2), kind=kLoop, calls=%fused_computation.2.clone.1 | loop fusion | flops 12451840 | bytes 557056 | tf_op jit(solution)/shard_map/while/body/eval_jaxpr/reduce_sum | solution.py:21
  65.1 1.6 convolution_add_fusion.2
  66.7 2.8 %convert_reduce_fusion.2 = f32[256,512]{1,0:T(8,128)S(1)} fusion(s32[256,32]{1,0:T(8,128)S(1)} %broadcast_subtract_fusion.2), kind=kLoop, calls=%fused_computation.2.clone.1 | loop fusion | flops 12451840 | bytes 557056 | tf_op jit(solution)/shard_map/while/body/eval_jaxpr/reduce_sum | solution.py:21
  69.5 1.6 convolution_add_fusion.2
  71.1 2.8 %convert_reduce_fusion.2 = f32[256,512]{1,0:T(8,128)S(1)} fusion(s32[256,32]{1,0:T(8,128)S(1)} %broadcast_subtract_fusion.2), kind=kLoop, calls=%fused_computation.2.clone.1 | loop fusion | flops 12451840 | bytes 557056 | tf_op jit(solution)/shard_map/while/body/eval_jaxpr/reduce_sum | solution.py:21
  73.9 1.6 convolution_add_fusion.2
  75.5 2.8 %convert_reduce_fusion.2 = f32[256,512]{1,0:T(8,128)S(1)} fusion(s32[256,32]{1,0:T(8,128)S(1)} %broadcast_subtract_fusion.2), kind=kLoop, calls=%fused_computation.2.clone.1 | loop fusion | flops 12451840 | bytes 557056 | tf_op jit(solution)/shard_map/while/body/eval_jaxpr/reduce_sum | solution.py:21
  78.3 1.6 convolution_add_fusion.2
  79.9 2.8 %convert_reduce_fusion.2 = f32[256,512]{1,0:T(8,128)S(1)} fusion(s32[256,32]{1,0:T(8,128)S(1)} %broadcast_subtract_fusion.2), kind=kLoop, calls=%fused_computation.2.clone.1 | loop fusion | flops 12451840 | bytes 557056 | tf_op jit(solution)/shard_map/while/body/eval_jaxpr/reduce_sum | solution.py:21
  82.7 1.6 convolution_add_fusion.2
  84.3 2.8 %convert_reduce_fusion.2 = f32[256,512]{1,0:T(8,128)S(1)} fusion(s32[256,32]{1,0:T(8,128)S(1)} %broadcast_subtract_fusion.2), kind=kLoop, calls=%fused_computation.2.clone.1 | loop fusion | flops 12451840 | bytes 557056 | tf_op jit(solution)/shard_map/while/body/eval_jaxpr/reduce_sum | solution.py:21
  87.1 1.6 convolution_add_fusion.2
  89.4 7.2 %all-to-all-done.1 = f32[1,8,128,512]{3,2,0,1:T(8,128)S(1)} async-done(((f32[1,8,128,512]{3,2,0,1:T(8,128)}), f32[1,8,128,512]{3,2,0,1:T(8,128)S(1)}, u32[]{:S(2)}, u32[]{:S(2)}) %all-to-all-start.1) | async-done | bytes 2097184 | tf_op jit(solution)/shard_map/all_to_all | solution.py:39
  96.6 56.6 %reduce-scatter.2.cloned.1.call-done = f32[32,128]{1,0:T(8,128)} async-done(((f32[256,128]{1,0:T(8,128)}), f32[32,128]{1,0:T(8,128)}) %reduce-scatter.2.cloned.1.call-update) | async-done | bytes 16400 | tf_op jit(solution)/shard_map/reduce_scatter | solution.py:51
  (18 shorter events, 2.1 us)
Async XLA Ops:
  7.2 4.3 %copy-start.1 = (s32[32,32]{1,0:T(8,128)S(1)}, s32[32,32]{1,0:T(8,128)}, u32[]{:S(2)}) copy-start(s32[32,32]{1,0:T(8,128)} %param.5) | copy-start | bytes 12292
  7.2 36.1 %all-to-all-start = ((f32[4,8,128,128]{3,2,1,0:T(8,128)}), f32[4,8,128,128]{3,2,1,0:T(8,128)S(1)}, u32[]{:S(2)}, u32[]{:S(2)}) async-start(f32[4,8,128,128]{3,2,1,0:T(8,128)} %bitcast.12), calls=%async_computation | async-start | bytes 4194304 | tf_op jit(solution)/shard_map/all_to_all | solution.py:40
  48.0 48.6 %all-to-all-start.1 = ((f32[1,8,128,512]{3,2,0,1:T(8,128)}), f32[1,8,128,512]{3,2,0,1:T(8,128)S(1)}, u32[]{:S(2)}, u32[]{:S(2)}) async-start(f32[1,8,128,512]{3,2,0,1:T(8,128)} %copy.8), calls=%async_computation.1 | async-start | bytes 4194304 | tf_op jit(solution)/shard_map/all_to_all | solution.py:39
  53.4 99.8 %reduce-scatter.2.cloned.1.call-start = ((), (), s32[]{:S(2)}) async-start(), calls=%async_computation.3 | async-start | bytes 147456 | tf_op jit(solution)/shard_map/reduce_scatter | solution.py:51
  88.7 0.7 copy-start
Sparse Core Ops, SparseCore 0:
  89.5 63.6 reduce-scatter.1
where the time goes:
time: 162 us; the launch traced here: 161 us
  waiting for transfers between devices  63.8 us (39%)
  blocking collectives  31.8 us (20%)
  other arithmetic  22.3 us (14%)
  between operations  14.1 us (9%)
  matrix products  12.6 us (8%)
  starting transfers between devices  9.69 us (6%)
  local copies, waits for them, and re-layouts  6.71 us (4%)
    reduce_scatter x1, waiting for transfers between devices, per_device(): lax.psum_scatter(pooling(positions, column_table), 'row', scatter_dimensi...  56.6 us
    all_gather x1, blocking collectives, per_device(): every_bag = lax.all_gather(bag_rows, 'row', axis=0, tiled=True)  31.8 us
    reduce_sum x8, other arithmetic, advance(): counts = jnp.sum(matches.astype(jnp.float32), axis=1)  22.2 us
    dot_general x8, matrix products, advance(): jnp.dot(counts, table_block, precision=lax.Precision.HIGHEST, preferred_e...  12.6 us
    all_to_all x1, waiting for transfers between devices, per_device(): lax.all_to_all(lax.all_to_all(sectioned, 'col', split_axis=0, concat_axis...  7.22 us
    all_to_all x1, starting transfers between devices, per_device(): lax.all_to_all(lax.all_to_all(sectioned, 'col', split_axis=0, concat_axis...  5.38 us
    all_to_all x2, local copies, waits for them, and re-layouts, per_device(): lax.all_to_all(sectioned, 'col', split_axis=0, concat_axis=3, tiled=True)  4.73 us
    all_to_all x1, starting transfers between devices, per_device(): lax.all_to_all(sectioned, 'col', split_axis=0, concat_axis=3, tiled=True)  4.28 us
  transfers between devices with their start and end apart: 3, of which 2 were waited for; matrix products, arithmetic and copies ran while one was open for 22% of the time, Pallas kernels for 0%

commit v1 on v0

v1 whole, which is shorter than its diff:
```python
import functools

import jax
import jax.numpy as jnp
from jax import lax
from jax.experimental import pallas as pl
from jax.experimental.pallas import tpu as pltpu
from jax.sharding import PartitionSpec as P

LANES = 128
SUB = 8
PACK = 2


def pool_kernel(first_ref, bags_ref, table_ref, out_ref, counts_ref):
    group_count, span = bags_ref.shape
    row_count, _ = table_ref.shape
    bag_len = span // SUB
    blocks = row_count // LANES
    first = first_ref[0]
    which = lax.broadcasted_iota(jnp.int32, (1, span), 1) // bag_len
    key_ids = lax.broadcasted_iota(jnp.int32, (blocks * SUB, span), 0)
    low_ids = lax.broadcasted_iota(jnp.int32, (LANES, span), 0)

    def count(index):
        within = bags_ref[pl.ds(index, 1), :] - first
        inside = (within >= 0) & (within < row_count)
        key = jnp.where(inside, (within >> 7) * SUB + which, -1)
        low = within & (LANES - 1)
        left = (key_ids == key).astype(jnp.float32).astype(jnp.bfloat16)
        right = (low_ids == low).astype(jnp.float32).astype(jnp.bfloat16)
        return lax.dot_general(
            left, right, (((1,), (1,)), ((), ())), preferred_element_type=jnp.float32
        )

    def fill(turn, _):
        parts = [count(turn * PACK + p) for p in range(PACK)]
        rows = pl.ds(pl.multiple_of(turn * PACK * SUB, PACK * SUB), PACK * SUB)
        for block in range(blocks):
            tile = jnp.concatenate(
                [part[block * SUB : (block + 1) * SUB, :] for part in parts], axis=0
            )
            counts_ref[rows, block * LANES : (block + 1) * LANES] = tile.astype(jnp.bfloat16)
        return 0

    lax.fori_loop(0, group_count // PACK, fill, 0)

    chunk = min(512, row_count)
    out_ref[...] = jnp.zeros_like(out_ref)

    def multiply(turn, _):
        place = pl.ds(pl.multiple_of(turn * chunk, chunk), chunk)
        rest = table_ref[place, :]
        left = counts_ref[:, place]
        total = out_ref[...]
        for _ in range(3):
            part = rest.astype(jnp.bfloat16)
            rest = rest - part.astype(jnp.float32)
            total += jnp.dot(left, part, preferred_element_type=jnp.float32)
        out_ref[...] = total
        return 0

    lax.fori_loop(0, row_count // chunk, multiply, 0)


def pool(first, bags, table):
    group_count, _ = bags.shape
    row_count, width = table.shape
    bag_count = group_count * SUB
    return pl.pallas_call(
        pool_kernel,
        out_shape=jax.ShapeDtypeStruct((bag_count, width), jnp.float32),
        in_specs=[
            pl.BlockSpec(memory_space=pltpu.SMEM),
            pl.BlockSpec(memory_space=pltpu.VMEM),
            pl.BlockSpec(memory_space=pltpu.VMEM),
        ],
        out_specs=pl.BlockSpec(memory_space=pltpu.VMEM),
        scratch_shapes=[pltpu.VMEM((bag_count, row_count), jnp.bfloat16)],
        cost_estimate=pl.CostEstimate(
            flops=20_000_000_000, bytes_accessed=4 * row_count * width, transcendentals=0
        ),
        name="pool",
    )(first, bags, table)


def place_kernel(cols, moved_ref, out_ref, sems):
    width = moved_ref.shape[-1]
    copies = []
    for c in range(cols):
        copies.append(
            pltpu.make_async_copy(
                moved_ref.at[c], out_ref.at[:, :, c * width : (c + 1) * width], sems.at[c]
            )
        )
    for copy in copies:
        copy.start()
    for copy in copies:
        copy.wait()


def place(moved):
    cols, rows, span, width = moved.shape
    if width % LANES:
        return moved.transpose(1, 2, 0, 3).reshape(rows, span, cols * width)
    return pl.pallas_call(
        functools.partial(place_kernel, cols),
        out_shape=jax.ShapeDtypeStruct((rows, span, cols * width), moved.dtype),
        in_specs=[pl.BlockSpec(memory_space=pl.ANY)],
        out_specs=pl.BlockSpec(memory_space=pl.ANY),
        scratch_shapes=[pltpu.SemaphoreType.DMA((cols,))],
        compiler_params=pltpu.CompilerParams(vmem_limit_bytes=1 << 20),
        name="place",
    )(moved)


def steps(column_table, bag_rows):
    rows = lax.axis_size("row")
    cols = lax.axis_size("col")
    block_len, width = column_table.shape
    own_bags, bag_len = bag_rows.shape
    span = block_len // (cols * rows)

    flat = bag_rows.reshape(1, own_bags // SUB, SUB * bag_len)
    every_bag = lax.all_to_all(
        jnp.broadcast_to(flat, (rows,) + flat.shape[1:]), "row", 0, 0, tiled=True
    ).reshape(rows * own_bags // SUB, SUB * bag_len)

    moved = lax.all_to_all(
        column_table.reshape(cols * rows, span, width), ("col", "row"), 0, 0, tiled=True
    )

    first = (lax.axis_index("row") * block_len).astype(jnp.int32).reshape(1)
    sums = pool(first, every_bag, column_table).reshape(rows, own_bags, width)
    pooled = jnp.sum(lax.all_to_all(sums, "row", 0, 0, tiled=True), axis=0)

    row_table = place(moved.reshape(cols, rows, span, width))
    return row_table, pooled


def solution(mesh):
    return jax.shard_map(
        steps,
        mesh=mesh,
        in_specs=(P("row", "col"), P("row", None)),
        out_specs=(P(None, ("col", "row"), None), P("row", "col")),
        check_vma=False,
    )
```

time: 162 us -> 90.7 us (0.56)
  other arithmetic: 22.3 us -> 0.62 us
  blocking collectives: 31.8 us -> 10.6 us
  between operations: 14.1 us -> 0.64 us
  matrix products: 12.6 us -> 0 us
  Pallas kernels: 0 us -> 10.4 us
  waiting for transfers between devices: 63.8 us -> 56 us
  local copies, waits for them, and re-layouts: 6.71 us -> 2.03 us
    reduce_scatter x1 -> x0, waiting for transfers between devices: 56.6 us -> none  [per_device(): lax.psum_scatter(pooling(positions, column_table), 'row', scatter_dimensi...]
    all_to_all x2, waiting for transfers between devices: 7.22 us -> 56 us  [the longest x1 49.3 us: steps(): lax.all_to_all(column_table.reshape(cols * rows, span, width), ('col', 'r...]
    all_gather x1 -> x0, blocking collectives: 31.8 us -> none  [per_device(): every_bag = lax.all_gather(bag_rows, 'row', axis=0, tiled=True)]
    reduce_sum x8 -> x1, other arithmetic: 22.2 us -> 0.62 us  [steps(): pooled = jnp.sum(lax.all_to_all(sums, 'row', 0, 0, tiled=True), axis=0)]
    dot_general x8 -> x0, matrix products: 12.6 us -> none  [advance(): jnp.dot(counts, table_block, precision=lax.Precision.HIGHEST, preferred_e...]
    all_to_all x0 -> x1, blocking collectives: none -> 10.6 us  [steps(): pooled = jnp.sum(lax.all_to_all(sums, 'row', 0, 0, tiled=True), axis=0)]
    pallas_call x0 -> x2, Pallas kernels: none -> 10.4 us  [the longest x1 9.04 us: pool(): pl.pallas_call(pool_kernel, out_shape=jax.ShapeDtypeStruct((bag_count, wi...]
    all_to_all x2 -> x0, local copies, waits for them, and re-layouts: 4.73 us -> none  [per_device(): lax.all_to_all(sectioned, 'col', split_axis=0, concat_axis=3, tiled=True)]
  transfers between devices with their start and end apart: 3 -> 2, of which waited for: 2 -> 2; matrix products, arithmetic and copies ran while one was open for 22% -> 1% of each run, Pallas kernels for 0% -> 0%
where the time goes in v1:
time: 90.7 us; the launch traced here: 90.3 us
  waiting for transfers between devices  56 us (62%)
  blocking collectives  10.6 us (12%)
  Pallas kernels  10.4 us (11%)
  starting transfers between devices  10 us (11%)
  local copies, waits for them, and re-layouts  2.03 us (2%)
    all_to_all x1, waiting for transfers between devices, steps(): lax.all_to_all(column_table.reshape(cols * rows, span, width), ('col', 'r...  49.3 us
    all_to_all x1, blocking collectives, steps(): pooled = jnp.sum(lax.all_to_all(sums, 'row', 0, 0, tiled=True), axis=0)  10.6 us
    pallas_call x1, Pallas kernels, pool(): pl.pallas_call(pool_kernel, out_shape=jax.ShapeDtypeStruct((bag_count, wi...  9.04 us
    all_to_all x1, starting transfers between devices, steps(): lax.all_to_all(jnp.broadcast_to(flat, (rows,) + flat.shape[1:]), 'row', 0...  7.28 us
    all_to_all x1, waiting for transfers between devices, steps(): lax.all_to_all(jnp.broadcast_to(flat, (rows,) + flat.shape[1:]), 'row', 0...  6.69 us
    all_to_all x1, starting transfers between devices, steps(): lax.all_to_all(column_table.reshape(cols * rows, span, width), ('col', 'r...  2.73 us
  transfers between devices with their start and end apart: 2, of which 2 were waited for; matrix products, arithmetic and copies ran while one was open for 1% of the time, Pallas kernels for 0%

profile of v1, /device:TPU:0, one launch (start us, length us, event | category | flops | bytes accessed | tf_op | source)
XLA Modules:
  0.0 90.3 jit_solution(12762899933252737470)
XLA Ops:
  0.6 0.8 broadcast_in_dim.7
  1.4 0.6 broadcast_in_dim.8
  2.0 7.3 %all-to-all-start.1 = ((s32[8,4,256]{2,1,0:T(4,128)}), s32[8,4,256]{2,1,0:T(4,128)S(1)}, u32[]{:S(2)}, u32[]{:S(2)}) async-start(s32[8,4,256]{2,1,0:T(4,128)} %broadcast_in_dim.8), calls=%async_computation.1 | async-start | bytes 65536 | tf_op jit(solution)/shard_map/all_to_all | solution.py:125
  9.3 6.7 %all-to-all-done.1 = s32[8,4,256]{2,1,0:T(4,128)S(1)} async-done(((s32[8,4,256]{2,1,0:T(4,128)}), s32[8,4,256]{2,1,0:T(4,128)S(1)}, u32[]{:S(2)}, u32[]{:S(2)}) %all-to-all-start.1) | async-done | bytes 32800 | tf_op jit(solution)/shard_map/all_to_all | solution.py:125
  16.0 0.6 reshape.24.bags_ref
  16.6 9.0 %pool.1 = f32[256,128]{1,0:T(8,128)} custom-call(s32[1]{0:T(128)} %bitcast.2.first_ref, s32[32,256]{1,0:T(8,128)} %reshape.24.bags_ref, f32[4096,128]{1,0:T(8,128)} %table_ref.1), custom_call_target="tpu_custom_call" | custom-call | flops 20000000000 | bytes 2097152 | tf_op jit(solution)/shard_map/pool/pallas_call | solution.py:70
  25.7 10.6 %all_to_all.15 = f32[8,32,128]{2,1,0:T(8,128)S(1)} all-to-all(f32[8,32,128]{2,1,0:T(8,128)} %bitcast.6), channel_id=1, replica_groups=mesh['col'=4,'row'=8] {'row'}, dimensions={0} | all-to-all | bytes 262144 | tf_op jit(solution)/shard_map/all_to_all | solution.py:135
  36.3 2.7 %all-to-all-start = ((f32[32,128,128]{2,1,0:T(8,128)}), f32[32,128,128]{2,1,0:T(8,128)S(1)}, u32[]{:S(2)}, u32[]{:S(2)}) async-start(f32[32,128,128]{2,1,0:T(8,128)} %bitcast.5), calls=%async_computation | async-start | bytes 4194304 | tf_op jit(solution)/shard_map/all_to_all | solution.py:129
  39.0 0.6 reduce_sum.9
  39.6 49.3 %all-to-all-done = f32[32,128,128]{2,1,0:T(8,128)S(1)} async-done(((f32[32,128,128]{2,1,0:T(8,128)}), f32[32,128,128]{2,1,0:T(8,128)S(1)}, u32[]{:S(2)}, u32[]{:S(2)}) %all-to-all-start) | async-done | bytes 2097184 | tf_op jit(solution)/shard_map/all_to_all | solution.py:129
  89.0 1.3 %place.1 = f32[8,128,512]{2,1,0:T(8,128)} custom-call(f32[4,8,128,128]{3,2,1,0:T(8,128)S(1)} %bitcast.4), custom_call_target="tpu_custom_call" | custom-call | tf_op jit(solution)/shard_map/place/pallas_call | solution.py:106
Async XLA Ops:
  2.0 14.0 %all-to-all-start.1 = ((s32[8,4,256]{2,1,0:T(4,128)}), s32[8,4,256]{2,1,0:T(4,128)S(1)}, u32[]{:S(2)}, u32[]{:S(2)}) async-start(s32[8,4,256]{2,1,0:T(4,128)} %broadcast_in_dim.8), calls=%async_computation.1 | async-start | bytes 65536 | tf_op jit(solution)/shard_map/all_to_all | solution.py:125
  36.3 52.7 %all-to-all-start = ((f32[32,128,128]{2,1,0:T(8,128)}), f32[32,128,128]{2,1,0:T(8,128)S(1)}, u32[]{:S(2)}, u32[]{:S(2)}) async-start(f32[32,128,128]{2,1,0:T(8,128)} %bitcast.5), calls=%async_computation | async-start | bytes 4194304 | tf_op jit(solution)/shard_map/all_to_all | solution.py:129
